TPU v7x, 256 devices: a whole 4x4x8 slice. The times are simulated.
256 devices in a mesh: dp: 16 (over x, z_hi, core), seq: 16 (over z_lo, y).
Axes of the slice: x: 4, y: 4, z: 8 (z_hi: 2, z_lo: 4; z = z_hi * 4 + z_lo), core: 2. Of those that a mesh axis runs over, the one named last changes fastest.
Arguments:
- tokens: bfloat16 [32, 2304, 1280], P('dp', 'seq'), may hold values from -60 to 60
- pre_gain: float32 [1280], replicated, may hold values from 0.5 to 1.5
- pre_shift: float32 [1280], replicated, may hold values from -3 to 3
- w_qkv: bfloat16 [1280, 3840], P('dp'), may hold values from -4 to 4
- qkv_bias: float32 [3840], replicated, may hold values from -3 to 3
- w_out: bfloat16 [1280, 1280], P('dp'), may hold values from -0.15625 to 0.15625
- out_bias: float32 [1280], replicated, may hold values from -3 to 3
- mlp_gain: float32 [1280], replicated, may hold values from 0.5 to 1.5
- mlp_shift: float32 [1280], replicated, may hold values from -3 to 3
- w_up: bfloat16 [1280, 2560], P('dp'), may hold values from -0.15625 to 0.15625
- up_bias: float32 [2560], replicated, may hold values from -3 to 3
- w_down: bfloat16 [2560, 1280], P('dp'), may hold values from -0.125 to 0.125
- down_bias: float32 [1280], replicated, may hold values from -3 to 3
Outputs:
- layer_out: bfloat16 [32, 2304, 1280], P('dp', 'seq')
All inputs are finite; a program needn't handle non-finite values.
Results may differ from a plain program's by a relative error of at most 0.0039.
Values may be sent and summed in bfloat16 or wider, within the bound.
A program may use at most 128 MiB of HBM per device.

v0:
```python
import math

import jax
import jax.numpy as jnp
from jax import lax
from jax.sharding import PartitionSpec as P

HEADS = 16
HEAD_DIM = 80


EPSILON = 1e-05


def grouped_exchange(array, axis, split_dim, concat_dim, work, item_dim, out_dim):

    def moved(group):
        return lax.all_to_all(group, axis, split_axis=split_dim, concat_axis=concat_dim, tiled=True)

    items = jax.tree.leaves(array)[0].shape[item_dim]
    ends = [items * k // 2 for k in range(2 + 1)] if items % 2 == 0 else [0, items]
    groups = [
        jax.tree.map(lambda a: lax.slice_in_dim(a, low, high, axis=item_dim), array)
        for low, high in zip(ends, ends[1:])
    ]
    arrived = [moved(group) for group in groups]
    made = [work(group) for group in arrived]
    return jax.tree.map(lambda *parts: jnp.concatenate(parts, axis=out_dim), *made)


def normalize(features, gain, shift):
    average = jnp.mean(features, axis=-1, keepdims=True)
    centered = features - average
    spread = jnp.mean(centered * centered, axis=-1, keepdims=True)
    return centered * lax.rsqrt(spread + EPSILON) * gain + shift


def fold_rows(left_side, shard_piece):
    return jnp.dot(left_side, shard_piece, preferred_element_type=jnp.float32)


def query_block(length):
    block_rows = length
    while block_rows > 1024 and block_rows % 2 == 0:
        block_rows = block_rows // 2
    return block_rows


def attend_back(packed_items):
    count, length, heads_here, triple = packed_items.shape
    head_size = triple // 3
    block_rows = query_block(length)
    factor = 1.0 / math.sqrt(head_size)

    def one_picture(picture):
        key_rows = picture[:, :, head_size : 2 * head_size]
        value_rows = picture[:, :, 2 * head_size :]
        queries = picture[:, :, :head_size].reshape(
            length // block_rows, block_rows, heads_here, head_size
        )

        def one_block(query_rows):
            scores = (
                jnp.einsum("qhd,khd->hqk", query_rows, key_rows, preferred_element_type=jnp.float32)
                * factor
            )
            highest = jnp.max(scores, axis=-1, keepdims=True)
            weights = jnp.exp(scores - highest)
            probs = (weights / jnp.sum(weights, axis=-1, keepdims=True)).astype(jnp.bfloat16)
            mixed = jnp.einsum(
                "hqk,khd->qhd", probs, value_rows, preferred_element_type=jnp.float32
            )
            return mixed.astype(jnp.bfloat16)

        outputs = lax.map(one_block, queries)
        return outputs.reshape(length, heads_here * head_size)

    context = lax.map(one_picture, packed_items)
    return lax.all_to_all(context, "seq", split_axis=1, concat_axis=2, tiled=True)


def shards(
    tokens,
    pre_gain,
    pre_shift,
    w_qkv,
    qkv_bias,
    w_out,
    out_bias,
    mlp_gain,
    mlp_shift,
    w_up,
    up_bias,
    w_down,
    down_bias,
):
    images_here, tok_here, width = tokens.shape
    row_count = images_here * tok_here
    triple = 3 * HEAD_DIM
    residual = tokens.reshape(row_count, width).astype(jnp.float32)
    normed = normalize(residual, pre_gain, pre_shift).astype(jnp.bfloat16)
    projected = fold_rows(normed, lax.all_gather(w_qkv, "dp", axis=0, tiled=True))
    packed = (
        (projected + qkv_bias).astype(jnp.bfloat16).reshape(images_here, tok_here, HEADS, triple)
    )
    context = grouped_exchange(packed, "seq", 2, 1, attend_back, 0, 0)
    context = context.reshape(row_count, width)
    attended = fold_rows(context, lax.all_gather(w_out, "dp", axis=0, tiled=True))
    middle = residual + attended + out_bias
    normed_mlp = normalize(middle, mlp_gain, mlp_shift).astype(jnp.bfloat16)
    lifted = fold_rows(normed_mlp, lax.all_gather(w_up, "dp", axis=0, tiled=True))
    hidden = jax.nn.gelu(lifted + up_bias, approximate=False).astype(jnp.bfloat16)
    lowered = fold_rows(hidden, lax.all_gather(w_down, "dp", axis=0, tiled=True))
    result = (middle + lowered + down_bias).astype(jnp.bfloat16)
    return result.reshape(images_here, tok_here, width)


def solution(mesh):
    in_specs = (
        P("dp", "seq", None),
        P(),
        P(),
        P("dp", None),
        P(),
        P("dp", None),
        P(),
        P(),
        P(),
        P("dp", None),
        P(),
        P("dp", None),
        P(),
    )
    out_specs = P("dp", "seq", None)
    return jax.shard_map(shards, mesh=mesh, in_specs=in_specs, out_specs=out_specs, check_vma=False)
```

profile of v0, /device:TPU:1, one launch (start us, length us, event | category | flops | bytes accessed | tf_op | source)
XLA Modules:
  0.0 421.2 jit_solution(7809553857395419662)
XLA Ops:
  8.7 1.3 convert_reduce_fusion
  10.1 1.5 multiply_reduce_fusion.1
  12.8 120.5 %all-gather.5.cloned.1.call-done = bf16[1280,3840]{1,0:T(8,128)(2,1)} async-done(((bf16[80,3840]{1,0:T(8,128)(2,1)}), bf16[1280,3840]{1,0:T(8,128)(2,1)}) %all-gather.5.cloned.1.call-update) | async-done | bytes 9830416 | tf_op jit(solution)/shard_map/all_gather | solution.py:102
  133.3 7.1 %fusion.20 = bf16[288,3840]{1,0:T(8,128)(2,1)S(1)} fusion(bf16[288,1280]{1,0:T(8,128)(2,1)S(1)} %fusion.37, bf16[1280,3840]{1,0:T(8,128)(2,1)} %all-gather.5.cloned.1.call-done, f32[3840]{0:T(1024)S(1)} %copy-done.1), kind=kOutput, calls=%fused_computation.27 | convolution fusion | flops 2833367040 | bytes 12794880 | tf_op jit(solution)/shard_map/dot_general | solution.py:39
  141.5 2.8 slice.37
  144.3 1.5 copy.40
  145.8 4.1 all-to-all-start
  150.5 3.7 slice.42
  154.1 1.4 copy.48
  155.6 20.2 %all-to-all-done = bf16[1,144,16,240]{3,1,0,2:T(8,128)(2,1)S(1)} async-done(((bf16[1,144,16,240]{3,1,0,2:T(8,128)(2,1)}), bf16[1,144,16,240]{3,1,0,2:T(8,128)(2,1)S(1)}, u32[]{:S(2)}, u32[]{:S(2)}) %all-to-all-start) | async-done | bytes 1105952 | tf_op jit(solution)/shard_map/all_to_all | solution.py:18
  175.8 25.8 %all-to-all-start.2 = ((bf16[1,144,16,240]{3,1,0,2:T(8,128)(2,1)}), bf16[1,144,16,240]{3,1,0,2:T(8,128)(2,1)S(1)}, u32[]{:S(2)}, u32[]{:S(2)}) async-start(bf16[1,144,16,240]{3,1,0,2:T(8,128)(2,1)} %copy.48), calls=%async_computation.2 | async-start | bytes 2359296 | tf_op jit(solution)/shard_map/all_to_all | solution.py:18
  201.6 1.6 fusion.110
  203.2 1.3 copy.41
  204.5 1.3 copy.42
  205.8 1.3 copy.43
  207.2 12.2 %while.34 = (s32[]{:T(128)}, bf16[4,576,1,80]{1,3,2,0:T(8,128)(2,1)S(1)}, bf16[4,576,1,80]{1,3,2,0:T(8,128)(2,1)S(1)}, bf16[2304,1,80]{0,2,1:T(8,128)(2,1)S(1)}, bf16[2304,1,80]{0,2,1:T(8,128)(2,1)S(1)}, /*index=5*/s32[]{:T(128)}) while((s32[]{:T(128)}, bf16[4,576,1,80]{1,3,2,0:T(8,128)(2,1)S(1)}, bf16[4,576,1,80]{1,3,2,0:T(8,128)(2,1)S(1)}, ...), condition=%wide.region_5.0_spmd, body=%wide.region_2.5_spmd.sunk | while | flops 434007936 | bytes 16882508 | solution.py:75
  220.4 3.5 reshape.145
  224.4 13.6 %reduce.11 = bf16[2304,80]{1,0:T(8,128)(2,1)} reduce(bf16[2304,1,80]{2,1,0:T(2,128)(2,1)S(1)} %bitcast.118, bf16[]{:T(256)} %broadcast.108), dimensions={1}, to_apply=%bitcast.83.reduce_sub_computation | reduce | bytes 737282
  238.0 2.8 reshape.149
  240.9 7.3 %all-to-all-start.1 = ((bf16[16,2,5760]{2,1,0:T(2,128)(2,1)}), bf16[16,2,5760]{2,1,0:T(2,128)(2,1)S(1)}, u32[]{:S(2)}, u32[]{:S(2)}) async-start(bf16[16,2,5760]{2,1,0:T(2,128)(2,1)} %reshape.149), calls=%async_computation.1 | async-start | bytes 737280 | tf_op jit(solution)/shard_map/all_to_all | solution.py:79
  249.4 1.3 copy.49
  251.2 12.2 %while.35 = (s32[]{:T(128)}, bf16[4,576,1,80]{1,3,2,0:T(8,128)(2,1)S(1)}, bf16[4,576,1,80]{1,3,2,0:T(8,128)(2,1)S(1)}, bf16[2304,1,80]{0,2,1:T(8,128)(2,1)S(1)}, bf16[2304,1,80]{0,2,1:T(8,128)(2,1)S(1)}, /*index=5*/s32[]{:T(128)}) while((s32[]{:T(128)}, bf16[4,576,1,80]{1,3,2,0:T(8,128)(2,1)S(1)}, bf16[4,576,1,80]{1,3,2,0:T(8,128)(2,1)S(1)}, ...), condition=%wide.region_9.10_spmd, body=%wide.region_6.0_spmd.sunk | while | flops 434007936 | bytes 16882508 | solution.py:75
  264.0 12.8 %reduce.10 = bf16[2304,80]{1,0:T(8,128)(2,1)S(1)} reduce(bf16[2304,1,80]{2,1,0:T(2,128)(2,1)S(1)} %bitcast.119, bf16[]{:T(256)} %broadcast.108), dimensions={1}, to_apply=%bitcast.81.reduce_sub_computation | reduce | bytes 737282
  276.8 1.8 reshape.147
  278.6 20.6 %all-to-all-start.3 = ((bf16[16,2,5760]{2,1,0:T(2,128)(2,1)}), bf16[16,2,5760]{2,1,0:T(2,128)(2,1)S(1)}, u32[]{:S(2)}, u32[]{:S(2)}) async-start(bf16[16,2,5760]{2,1,0:T(2,128)(2,1)} %reshape.147), calls=%async_computation.3 | async-start | bytes 737280 | tf_op jit(solution)/shard_map/all_to_all | solution.py:79
  299.2 1.3 reshape.150
  300.5 1.5 copy.46
  304.7 5.8 %all-to-all-done.3 = bf16[16,2,5760]{2,1,0:T(2,128)(2,1)S(1)} async-done(((bf16[16,2,5760]{2,1,0:T(2,128)(2,1)}), bf16[16,2,5760]{2,1,0:T(2,128)(2,1)S(1)}, u32[]{:S(2)}, u32[]{:S(2)}) %all-to-all-start.3) | async-done | bytes 368672 | tf_op jit(solution)/shard_map/all_to_all | solution.py:79
  311.7 1.7 copy.54
  316.3 3.3 fusion.112
  320.0 79.2 %all-gather.9.cloned.1.call-done = bf16[1280,2560]{1,0:T(8,128)(2,1)} async-done(((bf16[80,2560]{1,0:T(8,128)(2,1)}), bf16[1280,2560]{1,0:T(8,128)(2,1)}) %all-gather.9.cloned.1.call-update) | async-done | bytes 6553616 | tf_op jit(solution)/shard_map/all_gather | solution.py:111
  399.3 14.9 %fusion.33 = bf16[288,1280]{1,0:T(8,128)(2,1)} fusion(f32[288,1280]{1,0:T(8,128)S(1)} %get-tuple-element.142, bf16[2560,1280]{1,0:T(8,128)(2,1)} %all-gather.11.cloned.1.call-done, bf16[1280,2560]{1,0:T(8,128)(2,1)} %all-gather.9.cloned.1.call-done, f32[2560]{0:T(1024)S(1)} %copy-done.2, f32[1280]{0:T(1024)S(1)} %copy-done.4, f32[1280]{0:T(1024)S(1)} %copy-done.5, ...), kind=kOutput, calls=%fused_computation.52 | convolution fusion | flops 3826483200 | bytes 15346944 | tf_op jit(solution)/shard_map/dot_general | solution.py:39
  (76 shorter events, 40.3 us)
Async XLA Ops:
  6.5 5.1 %copy-start = (bf16[2,144,1280]{2,1,0:T(8,128)(2,1)S(1)}, bf16[2,144,1280]{2,1,0:T(8,128)(2,1)}, u32[]{:S(2)}) copy-start(bf16[2,144,1280]{2,1,0:T(8,128)(2,1)} %param.17) | copy-start | bytes 2211844
  6.5 126.7 %copy-start.1 = (f32[3840]{0:T(1024)S(1)}, f32[3840]{0:T(1024)}, u32[]{:S(2)}) copy-start(f32[3840]{0:T(1024)} %param.21) | copy-start | bytes 46084
  6.5 126.7 %all-gather.5.cloned.1.call-start = ((), (), s32[]{:S(2)}) async-start(), calls=%async_computation.4 | async-start | bytes 10444800 | tf_op jit(solution)/shard_map/all_gather | solution.py:102
  7.3 309.0 %all-gather.7.cloned.1.call-start = ((), (), s32[]{:S(2)}) async-start(), calls=%async_computation.5 | async-start | bytes 3481600 | tf_op jit(solution)/shard_map/all_gather | solution.py:108
  8.0 312.0 %all-gather.11.cloned.1.call-start = ((), (), s32[]{:S(2)}) async-start(), calls=%async_computation.7 | async-start | bytes 6963200 | tf_op jit(solution)/shard_map/all_gather | solution.py:113
  145.8 30.0 %all-to-all-start = ((bf16[1,144,16,240]{3,1,0,2:T(8,128)(2,1)}), bf16[1,144,16,240]{3,1,0,2:T(8,128)(2,1)S(1)}, u32[]{:S(2)}, u32[]{:S(2)}) async-start(bf16[1,144,16,240]{3,1,0,2:T(8,128)(2,1)} %copy.40), calls=%async_computation | async-start | bytes 2359296 | tf_op jit(solution)/shard_map/all_to_all | solution.py:18
  149.9 249.4 %all-gather.9.cloned.1.call-start = ((), (), s32[]{:S(2)}) async-start(), calls=%async_computation.6 | async-start | bytes 6963200 | tf_op jit(solution)/shard_map/all_gather | solution.py:111
  175.8 65.1 %all-to-all-start.2 = ((bf16[1,144,16,240]{3,1,0,2:T(8,128)(2,1)}), bf16[1,144,16,240]{3,1,0,2:T(8,128)(2,1)S(1)}, u32[]{:S(2)}, u32[]{:S(2)}) async-start(bf16[1,144,16,240]{3,1,0,2:T(8,128)(2,1)} %copy.48), calls=%async_computation.2 | async-start | bytes 2359296 | tf_op jit(solution)/shard_map/all_to_all | solution.py:18
  240.9 37.7 %all-to-all-start.1 = ((bf16[16,2,5760]{2,1,0:T(2,128)(2,1)}), bf16[16,2,5760]{2,1,0:T(2,128)(2,1)S(1)}, u32[]{:S(2)}, u32[]{:S(2)}) async-start(bf16[16,2,5760]{2,1,0:T(2,128)(2,1)} %reshape.149), calls=%async_computation.1 | async-start | bytes 737280 | tf_op jit(solution)/shard_map/all_to_all | solution.py:79
  278.6 31.8 %all-to-all-start.3 = ((bf16[16,2,5760]{2,1,0:T(2,128)(2,1)}), bf16[16,2,5760]{2,1,0:T(2,128)(2,1)S(1)}, u32[]{:S(2)}, u32[]{:S(2)}) async-start(bf16[16,2,5760]{2,1,0:T(2,128)(2,1)} %reshape.147), calls=%async_computation.3 | async-start | bytes 737280 | tf_op jit(solution)/shard_map/all_to_all | solution.py:79
  311.7 4.6 %copy-start.3 = (f32[1280]{0:T(1024)S(1)}, f32[1280]{0:T(1024)}, u32[]{:S(2)}) copy-start(f32[1280]{0:T(1024)} %param.23) | copy-start | bytes 15364
  316.3 83.0 %copy-start.2 = (f32[2560]{0:T(1024)S(1)}, f32[2560]{0:T(1024)}, u32[]{:S(2)}) copy-start(f32[2560]{0:T(1024)} %param.27) | copy-start | bytes 30724
  316.3 83.0 %copy-start.4 = (f32[1280]{0:T(1024)S(1)}, f32[1280]{0:T(1024)}, u32[]{:S(2)}) copy-start(f32[1280]{0:T(1024)} %param.29) | copy-start | bytes 15364
  316.3 83.0 %copy-start.5 = (f32[1280]{0:T(1024)S(1)}, f32[1280]{0:T(1024)}, u32[]{:S(2)}) copy-start(f32[1280]{0:T(1024)} %param.25) | copy-start | bytes 15364
  316.3 83.0 %copy-start.6 = (f32[1280]{0:T(1024)S(1)}, f32[1280]{0:T(1024)}, u32[]{:S(2)}) copy-start(f32[1280]{0:T(1024)} %param.24) | copy-start | bytes 15364
Sparse Core Ops, SparseCore 0:
  10.0 123.1 all-gather.4
  135.9 59.7 all-gather.6
  198.5 104.8 all-gather.10
  305.9 93.3 all-gather.8
where the time goes:
time: 427 us; the launch traced here: 421 us
  waiting for transfers between devices  228 us (53%)
  starting transfers between devices  57.9 us (14%)
  matrix products  42.5 us (10%)
  local copies, waits for them, and re-layouts  40.8 us (10%)
  other arithmetic  37.6 us (9%)
  between operations  13.9 us (3%)
    all_gather x1, waiting for transfers between devices, shards(): lax.all_gather(w_qkv, 'dp', axis=0, tiled=True)  120 us
    all_gather x1, waiting for transfers between devices, shards(): lax.all_gather(w_up, 'dp', axis=0, tiled=True)  79.2 us
    all_to_all x2, starting transfers between devices, moved(): lax.all_to_all(group, axis, split_axis=split_dim, concat_axis=concat_dim,...  29.9 us
    all_to_all x2, starting transfers between devices, attend_back(): lax.all_to_all(context, 'seq', split_axis=1, concat_axis=2, tiled=True)  27.8 us
    unnamed x2, other arithmetic  26.4 us
    dot_general x3, matrix products, fold_rows(): return jnp.dot(left_side, shard_piece, preferred_element_type=jnp.float32)  25.3 us
    all_to_all x2, waiting for transfers between devices, moved(): lax.all_to_all(group, axis, split_axis=split_dim, concat_axis=concat_dim,...  20.2 us
    slice x5, local copies, waits for them, and re-layouts, grouped_exchange(): lax.slice_in_dim(a, low, high, axis=item_dim)  10.5 us
  transfers between devices with their start and end apart: 8, of which 4 were waited for; matrix products, arithmetic and copies ran while one was open for 24% of the time, Pallas kernels for 0%

commit v1 on v0

v1 whole, which is shorter than its diff:
```python
import math

import jax
import jax.numpy as jnp
from jax import lax
from jax.experimental import pallas as pl
from jax.experimental.pallas import tpu as pltpu
from jax.sharding import PartitionSpec as P

D = 1280
HEADS = 16
HEAD_DIM = 80
FF = 2560
TOK = 144
SEQ = 2304
HALF = 1920
PAIR = 480
EPSILON = 1e-05
EXP_SCALE = math.log2(math.e) / math.sqrt(HEAD_DIM)

MESH = pl.DeviceIdType.MESH
F32 = jnp.float32
BF16 = jnp.bfloat16

COLS = (HALF, D, FF, D)
LOW = (1024, 640, 1280, 640)
ROWS = (80, 80, 80, 160)
XM, XP, X2L, X2R, ZC, YC, DC = 0, 1, 2, 3, 8, 9, 10


def kernel(
    x_ref, pre_gain, pre_shift, qkv_bias, out_bias, mlp_gain, mlp_shift, up_bias, down_bias,
    wqkv_in, wout_in, wup_in, wdown_in,
    o_ref,
    wqkv, wout, wup, wdown,
    tok, other, packed, qsend, qin, qb, kb, vb, csend, cin, zsend, ctx, mid, normed_mlp, hid,
    load_sem, w_send, w_recv, t_send, t_recv, y_send, y_recv, c_send, c_recv, z_send, z_recv,
):
    dp = lax.axis_index("dp")
    sq = lax.axis_index("seq")
    x, zh, c = dp // 4, (dp // 2) % 2, dp % 2
    zl, y = sq // 4, sq % 4
    half, part = zl // 2, zl % 2

    def dev(x=x, zh=zh, c=c, zl=zl, y=y):
        return ((x * 2 + zh) * 2 + c, zl * 4 + y)

    xr, xl, xo = (x + 1) % 4, (x + 3) % 4, (x + 2) % 4
    ypair = y + 1 - 2 * (y % 2)
    partner = zl + 1 - 2 * part
    near_here = 1 + half
    is_near = zl == near_here
    near_other = 2 - half
    far_other = 3 - 3 * half

    barrier = pltpu.get_barrier_semaphore()
    peers = [dev(x=xr), dev(x=xl), dev(zh=1 - zh), dev(c=1 - c)]
    peers += [dev(zl=(zl + d) % 4) for d in (1, 2, 3)]
    peers += [dev(y=(y + d) % 4) for d in (1, 2, 3)]

    bufs = (wqkv, wout, wup, wdown)
    sources = (
        wqkv_in.at[:, pl.ds(pl.multiple_of(part * HALF, 128), HALF)],
        wout_in,
        wup_in,
        wdown_in,
    )
    loads = [
        pltpu.make_async_copy(sources[i], bufs[i].at[x, zh, c], load_sem.at[i]) for i in range(4)
    ]
    for load in loads:
        load.start()
    for peer in peers:
        pl.semaphore_signal(barrier, inc=1, device_id=peer, device_id_type=MESH)
    pl.semaphore_wait(barrier, len(peers))

    started = []

    def region(i, xx, zz, cc, lo=0, size=None):
        size = COLS[i] if size is None else size
        return bufs[i].at[xx, zz, cc, :, pl.ds(lo, size)]

    def w_copy(i, j, ref, target):
        return pltpu.make_async_remote_copy(
            src_ref=ref, dst_ref=ref, send_sem=w_send.at[i, j], recv_sem=w_recv.at[i, j],
            device_id=target, device_id_type=MESH,
        )

    def w_start(i, j, ref, target):
        copy = w_copy(i, j, ref, target)
        copy.start()
        started.append(copy)

    def w_wait(i, j, ref):
        w_copy(i, j, ref, dev(c=1 - c)).wait_recv()

    def side(k):
        return zh if k == 0 else 1 - zh

    def ring_start(i, k):
        mine = region(i, x, side(k), c)
        w_start(i, 4 * k + XM, mine, dev(x=xr))
        w_start(i, 4 * k + XP, mine, dev(x=xl))

    def ring_relay(i, k):
        low, high = LOW[i], COLS[i] - LOW[i]
        w_wait(i, 4 * k + XM, region(i, xl, side(k), c))
        w_start(i, 4 * k + X2L, region(i, xl, side(k), c, 0, low), dev(x=xr))
        w_wait(i, 4 * k + XP, region(i, xr, side(k), c))
        w_start(i, 4 * k + X2R, region(i, xr, side(k), c, low, high), dev(x=xl))

    def ring_end(i, k):
        low, high = LOW[i], COLS[i] - LOW[i]
        w_wait(i, 4 * k + X2L, region(i, xo, side(k), c, 0, low))
        w_wait(i, 4 * k + X2R, region(i, xo, side(k), c, low, high))
        w_start(i, DC + k, bufs[i].at[:, side(k), c], dev(c=1 - c))

    def sibling_wait(i, k):
        w_wait(i, DC + k, bufs[i].at[:, side(k), 1 - c])

    def cut(i, which):
        size = LOW[i]
        return pl.multiple_of(which * size, 128), size

    def class_start(i):
        if i == 0:
            w_start(i, ZC, region(i, x, zh, c), dev(zh=1 - zh))
        else:
            lo, size = cut(i, y % 2)
            w_start(i, ZC, region(i, x, zh, c, lo, size), dev(zh=1 - zh))

    def class_swap(i):
        lo, size = cut(i, y % 2)
        w_wait(i, ZC, region(i, x, 1 - zh, c, lo, size))
        w_start(i, YC, region(i, x, 1 - zh, c, lo, size), dev(y=ypair))

    def class_ring(i):
        if i == 0:
            w_wait(i, ZC, region(i, x, 1 - zh, c))
        else:
            lo, size = cut(i, 1 - y % 2)
            w_wait(i, YC, region(i, x, 1 - zh, c, lo, size))
        ring_start(i, 1)

    loads[0].wait()
    class_start(0)
    ring_start(0, 0)

    def norm_rows(rows, gain, shift):
        average = jnp.mean(rows, axis=-1, keepdims=True)
        centered = rows - average
        spread = jnp.mean(centered * centered, axis=-1, keepdims=True)
        return centered * lax.rsqrt(spread + EPSILON) * gain[...] + shift[...]

    def norm_image(image, store):
        @pl.loop(0, TOK // 16)
        def _(n):
            at = pl.ds(pl.multiple_of(n * 16, 16), 16)
            rows = x_ref[image, at, :].astype(F32)
            store(at, norm_rows(rows, pre_gain, pre_shift).astype(BF16))

    def store_other(at, value):
        other[at, :] = value

    def store_own(at, value):
        tok[zl, at, :] = value

    def t_copy(src, slot, j, target):
        return pltpu.make_async_remote_copy(
            src_ref=src, dst_ref=tok.at[slot], send_sem=t_send.at[j], recv_sem=t_recv.at[slot],
            device_id=target, device_id_type=MESH,
        )

    norm_image(1 - half, store_other)
    to_near = t_copy(other, zl, 1, dev(zl=near_other))
    to_near.start()
    to_far = t_copy(other, zl, 2, dev(zl=far_other))

    @pl.when(is_near)
    def _():
        to_far.start()

    norm_image(half, store_own)
    to_partner = t_copy(tok.at[zl], zl, 0, dev(zl=partner))
    to_partner.start()

    for load in loads[1:]:
        load.wait()

    class_ring(0)
    ring_relay(0, 0)
    for i in (1, 2, 3):
        ring_start(i, 0)
    onward = t_copy(tok.at[far_other], far_other, 3, dev(zl=partner))

    def token_wait(slot):
        t_copy(tok.at[slot], slot, 0, dev(zl=partner)).wait_recv()

    ring_end(0, 0)
    ring_relay(0, 1)

    @pl.when(is_near)
    def _():
        token_wait(far_other)
        onward.start()

    ring_end(0, 1)
    sibling_wait(0, 0)
    sibling_wait(0, 1)

    def slot_of(j):
        last = jnp.where(j == 2, near_other, far_other)
        return jnp.where(j == 0, zl, jnp.where(j == 1, partner, last))

    def y_copy(r, slot):
        to = (y + r) % 4
        return pltpu.make_async_remote_copy(
            src_ref=qsend.at[to, slot], dst_ref=qin.at[y, slot],
            send_sem=y_send.at[r - 1, slot], recv_sem=y_recv.at[r - 1, slot],
            device_id=dev(y=to), device_id_type=MESH,
        )

    @pl.loop(0, 4)
    def _(j):
        slot = slot_of(j)

        @pl.when((j > 0) & jnp.logical_not((j == 3) & is_near))
        def _():
            token_wait(slot)

        rows = tok[slot]
        for n in range(3):
            at = slice(640 * n, 640 * n + 640)
            block = wqkv[:, :, :, :, at].reshape(D, 640)
            packed[:, at] = jnp.dot(rows, block, preferred_element_type=F32) + qkv_bias[part, :, at]
        for to in range(4):
            start = PAIR * to // 128 * 128
            wide = packed[:, start : min(start + 640, HALF)]
            shift = PAIR * to - start
            if shift:
                wide = pltpu.roll(wide, wide.shape[1] - shift, 1)
            qsend[to, slot] = wide[:, :512].astype(BF16)
        qin[y, slot] = qsend[y, slot]
        for r in (2, 1, 3):
            y_copy(r, slot).start()

    for i in (1, 2, 3):
        class_start(i)
        ring_relay(i, 0)

    def y_copy_in(r, slot, source):
        return pltpu.make_async_remote_copy(
            src_ref=qin.at[source, slot], dst_ref=qin.at[source, slot],
            send_sem=y_send.at[r - 1, slot], recv_sem=y_recv.at[r - 1, slot],
            device_id=dev(y=(y + 1) % 4), device_id_type=MESH,
        )

    lane128 = lax.broadcasted_iota(jnp.int32, (TOK, 128), 1)
    lane256 = lax.broadcasted_iota(jnp.int32, (TOK, 256), 1)

    @pl.loop(0, 16)
    def _(n):
        j, r = n // 4, n % 4
        slot = slot_of(j)
        source = (y + 4 - r) % 4

        @pl.when(r > 0)
        def _():
            y_copy_in(r, slot, source).wait_recv()

        wide = qin[source, slot].astype(F32)
        at = pl.ds(pl.multiple_of((source * 4 + slot) * TOK, 16), TOK)
        keep = lane128 < HEAD_DIM
        k0 = pltpu.roll(wide, 512 - 80, 1)
        v0 = pltpu.roll(wide, 512 - 160, 1)
        q1 = pltpu.roll(wide, 512 - 240, 1)
        k1 = pltpu.roll(wide, 512 - 320, 1)
        qb[0, at, :] = jnp.where(keep, wide[:, :128], 0.0).astype(BF16)
        qb[1, at, :] = jnp.where(keep, q1[:, :128], 0.0).astype(BF16)
        kb[0, at, :] = jnp.where(keep, k0[:, :128], 0.0).astype(BF16)
        kb[1, at, :] = jnp.where(keep, k1[:, :128], 0.0).astype(BF16)
        ones = jnp.where(lane256 == 160, 1.0, 0.0)
        vb[0, at, :] = jnp.where(lane256 < 80, v0[:, :256], ones).astype(BF16)
        in_second = (lane256 >= 80) & (lane256 < 160)
        vb[1, at, :] = jnp.where(in_second, k1[:, :256], ones).astype(BF16)

    for i in (1, 2, 3):
        ring_end(i, 0)
    for i in (1, 2, 3):
        class_swap(i)

    def c_copy(t, r):
        to = (y + r) % 4
        return pltpu.make_async_remote_copy(
            src_ref=csend.at[to], dst_ref=cin.at[y],
            send_sem=c_send.at[t], recv_sem=c_recv.at[t],
            device_id=dev(y=to), device_id_type=MESH,
        )

    def c_wait(t, r):
        source = (y + 4 - r) % 4
        pltpu.make_async_remote_copy(
            src_ref=cin.at[source], dst_ref=cin.at[source],
            send_sem=c_send.at[t], recv_sem=c_recv.at[t],
            device_id=dev(y=(y + 1) % 4), device_id_type=MESH,
        ).wait_recv()

    def attend(to, n):
        at = pl.ds(pl.multiple_of((to * 4 + n) * TOK, 16), TOK)
        sums = []
        for head in range(2):
            scores = lax.dot_general(
                qb[head, at, :], kb[head], (((1,), (1,)), ((), ())), preferred_element_type=F32
            )
            highest = jnp.max(scores, axis=-1, keepdims=True) * EXP_SCALE
            weights = jnp.exp2(scores * EXP_SCALE - highest).astype(BF16)
            total = jnp.dot(weights, vb[head], preferred_element_type=F32)
            sums.append(total / total[:, 160:161])
        mixed = jnp.where(lane256 < 80, sums[0], jnp.where(lane256 < 160, sums[1], 0.0))
        csend[to, pl.ds(pl.multiple_of(n * TOK, 16), TOK), :] = mixed.astype(BF16)

    order = (2, 1, 3, 0)
    for t, r in enumerate(order):
        to = (y + r) % 4

        @pl.loop(0, 4)
        def _(n):
            attend(to, n)

        if r:
            c_copy(t, r).start()
        if t == 0:
            for i in (1, 2, 3):
                class_ring(i)
        if t == 2:
            ring_relay(1, 1)
        if t == 3:
            ring_relay(2, 1)

    cin[y] = csend[y]
    for t, r in enumerate(order[:3]):
        c_wait(t, r)

    def z_copy(d):
        to = (zl + d) % 4
        return pltpu.make_async_remote_copy(
            src_ref=zsend.at[d],
            dst_ref=ctx.at[half, :, pl.ds(pl.multiple_of(640 * part, 128), 640)],
            send_sem=z_send.at[d], recv_sem=z_recv.at[d],
            device_id=dev(zl=to), device_id_type=MESH,
        )

    def z_wait(d):
        source = (zl + 4 - d) % 4
        ref = ctx.at[source // 2, :, pl.ds(pl.multiple_of(640 * (source % 2), 128), 640)]
        pltpu.make_async_remote_copy(
            src_ref=ref, dst_ref=ref, send_sem=z_send.at[d], recv_sem=z_recv.at[d],
            device_id=dev(zl=partner), device_id_type=MESH,
        ).wait_recv()

    for d in (2, 3, 1, 0):
        to = (zl + d) % 4
        at = pl.ds(pl.multiple_of(to * TOK, 16), TOK)
        joined = None
        for s in range(4):
            piece = cin[s, at, :].astype(F32)
            wide = jnp.concatenate([piece, jnp.zeros((TOK, 384), F32)], axis=1)
            if s:
                wide = pltpu.roll(wide, 160 * s, 1)
            joined = wide if joined is None else joined + wide
        if d:
            zsend[d] = joined.astype(BF16)
            z_copy(d).start()
        else:
            ctx[half, :, pl.ds(pl.multiple_of(640 * part, 128), 640)] = joined.astype(BF16)

    ring_relay(3, 1)
    for i in (1, 2, 3):
        ring_end(i, 1)
    for d in (1, 2, 3):
        z_wait(d)

    rows = 2 * TOK
    sibling_wait(1, 0)
    sibling_wait(1, 1)

    @pl.loop(0, 5)
    def _(n):
        at = pl.ds(pl.multiple_of(256 * n, 256), 256)
        block = wout[:, :, :, :, at].reshape(D, 256)
        made = jnp.dot(ctx[...].reshape(rows, D), block, preferred_element_type=F32)
        mid[:, at] = x_ref[:, :, at].reshape(rows, 256).astype(F32) + made + out_bias[:, at]

    @pl.loop(0, rows // 16)
    def _(n):
        at = pl.ds(pl.multiple_of(n * 16, 16), 16)
        normed_mlp[at, :] = norm_rows(mid[at, :], mlp_gain, mlp_shift).astype(BF16)

    sibling_wait(2, 0)
    sibling_wait(2, 1)

    @pl.loop(0, 10)
    def _(n):
        at = pl.ds(pl.multiple_of(256 * n, 256), 256)
        block = wup[:, :, :, :, at].reshape(D, 256)
        lifted = jnp.dot(normed_mlp[...], block, preferred_element_type=F32) + up_bias[:, at]
        hid[:, at] = (0.5 * lifted * (1.0 + lax.erf(lifted * math.sqrt(0.5)))).astype(BF16)

    sibling_wait(3, 0)
    sibling_wait(3, 1)

    @pl.loop(0, 5)
    def _(n):
        at = pl.ds(pl.multiple_of(256 * n, 256), 256)
        block = wdown[:, :, :, :, at].reshape(FF, 256)
        lowered = jnp.dot(hid[...], block, preferred_element_type=F32)
        result = mid[:, at] + lowered + down_bias[:, at]
        o_ref[:, :, at] = result.astype(BF16).reshape(2, TOK, 256)

    for copy in started:
        copy.wait_send()
    to_partner.wait_send()
    to_near.wait_send()

    @pl.when(is_near)
    def _():
        to_far.wait_send()
        onward.wait_send()

    @pl.loop(0, 4)
    def _(slot):
        for r in (1, 2, 3):
            y_copy(r, slot).wait_send()

    for t, r in enumerate(order[:3]):
        c_copy(t, r).wait_send()
    for d in (1, 2, 3):
        z_copy(d).wait_send()


def layer(
    tokens, pre_gain, pre_shift, w_qkv, qkv_bias, w_out, out_bias,
    mlp_gain, mlp_shift, w_up, up_bias, w_down, down_bias,
):
    vmem = pl.BlockSpec(memory_space=pltpu.VMEM)
    hbm = pl.BlockSpec(memory_space=pltpu.HBM)
    dma = pltpu.SemaphoreType.DMA
    return pl.pallas_call(
        kernel,
        out_shape=jax.ShapeDtypeStruct((2, TOK, D), BF16),
        in_specs=[vmem] * 9 + [hbm] * 4,
        out_specs=vmem,
        scratch_shapes=[
            pltpu.VMEM((4, 2, 2, 80, HALF), BF16),
            pltpu.VMEM((4, 2, 2, 80, D), BF16),
            pltpu.VMEM((4, 2, 2, 80, FF), BF16),
            pltpu.VMEM((4, 2, 2, 160, D), BF16),
            pltpu.VMEM((4, TOK, D), BF16),
            pltpu.VMEM((TOK, D), BF16),
            pltpu.VMEM((TOK, HALF), F32),
            pltpu.VMEM((4, 4, TOK, 512), BF16),
            pltpu.VMEM((4, 4, TOK, 512), BF16),
            pltpu.VMEM((2, SEQ, 128), BF16),
            pltpu.VMEM((2, SEQ, 128), BF16),
            pltpu.VMEM((2, SEQ, 256), BF16),
            pltpu.VMEM((4, 4 * TOK, 256), BF16),
            pltpu.VMEM((4, 4 * TOK, 256), BF16),
            pltpu.VMEM((4, TOK, 640), BF16),
            pltpu.VMEM((2, TOK, D), BF16),
            pltpu.VMEM((2 * TOK, D), F32),
            pltpu.VMEM((2 * TOK, D), BF16),
            pltpu.VMEM((2 * TOK, FF), BF16),
            dma((4,)), dma((4, 12)), dma((4, 12)), dma((4,)), dma((4,)),
            dma((3, 4)), dma((3, 4)), dma((3,)), dma((3,)), dma((4,)), dma((4,)),
        ],
        compiler_params=pltpu.CompilerParams(
            collective_id=0, has_side_effects=True, vmem_limit_bytes=67043328
        ),
    )(
        tokens, pre_gain[None], pre_shift[None], qkv_bias.reshape(2, 1, HALF), out_bias[None],
        mlp_gain[None], mlp_shift[None], up_bias[None], down_bias[None],
        w_qkv, w_out, w_up, w_down,
    )


def solution(mesh):
    in_specs = (
        P("dp", "seq", None),
        P(), P(), P("dp", None), P(), P("dp", None), P(), P(), P(), P("dp", None), P(),
        P("dp", None), P(),
    )
    out_specs = P("dp", "seq", None)
    return jax.shard_map(layer, mesh=mesh, in_specs=in_specs, out_specs=out_specs, check_vma=False)
```

time: 427 us -> 164 us (0.38)
  the two profiles are of different devices: /device:TPU:1 before, /device:TPU:33 now
where the time goes in v1:
time: 164 us
  Pallas kernels  156 us (95%)
  local copies, waits for them, and re-layouts  7.84 us (5%)
    pallas_call x1, Pallas kernels, layer(): pl.pallas_call(kernel, out_shape=jax.ShapeDtypeStruct((2, TOK, D), BF16),...  156 us

profile of v1, /device:TPU:33, one launch (start us, length us, event | category | flops | bytes accessed | tf_op | source)
XLA Modules:
  0.0 163.5 jit_solution(6347021269049988609)
XLA Ops:
  0.0 0.0 copy-start.2
  0.0 1.3 broadcast_in_dim.21.pre_gain
  1.3 0.0 copy-done.2
  1.3 0.0 copy-start.3
  1.3 0.6 broadcast_in_dim.22.pre_shift
  1.9 0.1 copy-done.3
  2.0 0.0 copy-start.4
  2.0 0.6 broadcast_in_dim.23.out_bias
  2.6 0.1 copy-done.4
  2.7 0.0 copy-start.5
  2.7 0.0 copy-start.6
  2.7 0.6 broadcast_in_dim.24.mlp_gain
  3.3 0.1 copy-done.5
  3.4 0.0 copy-start.1
  3.4 0.6 broadcast_in_dim.25.mlp_shift
  4.0 0.0 copy-done.6
  4.0 0.0 copy-start
  4.0 0.6 broadcast_in_dim.27.down_bias
  4.6 0.0 copy-done.1
  4.6 0.6 broadcast_in_dim.26.up_bias
  5.2 0.0 copy-done
  5.2 0.6 reshape.3.qkv_bias
  5.8 155.7 %shard_map.127 = bf16[2,144,1280]{2,1,0:T(8,128)(2,1)} custom-call(bf16[2,144,1280]{2,1,0:T(8,128)(2,1)} %x_ref.1, f32[1,1280]{1,0:T(1,128)} %broadcast_in_dim.21.pre_gain, f32[1,1280]{1,0:T(1,128)} %broadcast_in_dim.22.pre_shift, f32[2,1,1920]{2,1,0:T(1,128)} %reshape.3.qkv_bias, f32[1,1280]{1,0:T(1,128)} %broadcast_in_dim.23.out_bias, ...), custom_call_target="tpu_custom_call" | custom-call | tf_op jit(solution)/shard_map/pallas_call | solution.py:448
  161.5 2.0 %copy.15 = bf16[2,144,1280]{2,1,0:T(8,128)(2,1)} copy(bf16[2,144,1280]{2,1,0:T(8,128)(2,1)} %shard_map.127) | data formatting | bytes 1474560
Async XLA Ops:
  0.0 1.3 copy-start.2
  1.3 0.7 copy-start.3
  2.0 0.7 copy-start.4
  2.7 0.7 copy-start.5
  2.7 1.3 copy-start.6
  3.4 1.2 copy-start.1
  4.0 1.2 copy-start

commit v2 on v1

v2 whole, which is shorter than its diff:
```python
import math

import jax
import jax.numpy as jnp
from jax import lax
from jax.experimental import pallas as pl
from jax.experimental.pallas import tpu as pltpu
from jax.sharding import PartitionSpec as P

D = 1280
HEADS = 16
HEAD_DIM = 80
FF = 2560
TOK = 144
SEQ = 2304
HALF = 1920
PAIR = 480
EPSILON = 1e-05
EXP_SCALE = math.log2(math.e) / math.sqrt(HEAD_DIM)

MESH = pl.DeviceIdType.MESH
F32 = jnp.float32
BF16 = jnp.bfloat16

COLS = (HALF, D, FF, D)
LOW = (1024, 640, 1280, 640)
ROWS = (80, 80, 80, 160)
XM, XP, X2L, X2R, ZC, YC, DC = 0, 1, 2, 3, 8, 9, 10


def kernel(
    x_ref, pre_gain, pre_shift, qkv_bias, out_bias, mlp_gain, mlp_shift, up_bias, down_bias,
    wqkv_in, wout_in, wup_in, wdown_in,
    o_ref,
    wqkv, wout, wup, wdown,
    tok, other, packed, qsend, qin, qb, kb, vb, score_a, score_b, csend, cin, zsend, ctx, mid, normed_mlp, hid,
    load_sem, w_send, w_recv, t_send, t_recv, y_send, y_recv, c_send, c_recv, z_send, z_recv,
):
    dp = lax.axis_index("dp")
    sq = lax.axis_index("seq")
    x, zh, c = dp // 4, (dp // 2) % 2, dp % 2
    zl, y = sq // 4, sq % 4
    half, part = zl // 2, zl % 2

    def dev(x=x, zh=zh, c=c, zl=zl, y=y):
        return ((x * 2 + zh) * 2 + c, zl * 4 + y)

    xr, xl, xo = (x + 1) % 4, (x + 3) % 4, (x + 2) % 4
    ypair = y + 1 - 2 * (y % 2)
    partner = zl + 1 - 2 * part
    near_here = 1 + half
    is_near = zl == near_here
    near_other = 2 - half
    far_other = 3 - 3 * half

    barrier = pltpu.get_barrier_semaphore()
    peers = [dev(x=xr), dev(x=xl), dev(zh=1 - zh), dev(c=1 - c)]
    peers += [dev(zl=(zl + d) % 4) for d in (1, 2, 3)]
    peers += [dev(y=(y + d) % 4) for d in (1, 2, 3)]

    bufs = (wqkv, wout, wup, wdown)
    sources = (
        wqkv_in.at[:, pl.ds(pl.multiple_of(part * HALF, 128), HALF)],
        wout_in,
        wup_in,
        wdown_in,
    )
    loads = [
        pltpu.make_async_copy(sources[i], bufs[i].at[x, zh, c], load_sem.at[i]) for i in range(4)
    ]
    for load in loads:
        load.start()
    for peer in peers:
        pl.semaphore_signal(barrier, inc=1, device_id=peer, device_id_type=MESH)
    pl.semaphore_wait(barrier, len(peers))

    started = []

    def region(i, xx, zz, cc, lo=0, size=None):
        size = COLS[i] if size is None else size
        return bufs[i].at[xx, zz, cc, :, pl.ds(lo, size)]

    def w_copy(i, j, ref, target):
        return pltpu.make_async_remote_copy(
            src_ref=ref, dst_ref=ref, send_sem=w_send.at[i, j], recv_sem=w_recv.at[i, j],
            device_id=target, device_id_type=MESH,
        )

    def w_start(i, j, ref, target):
        copy = w_copy(i, j, ref, target)
        copy.start()
        started.append(copy)

    def w_wait(i, j, ref):
        w_copy(i, j, ref, dev(c=1 - c)).wait_recv()

    def side(k):
        return zh if k == 0 else 1 - zh

    def ring_start(i, k):
        mine = region(i, x, side(k), c)
        w_start(i, 4 * k + XM, mine, dev(x=xr))
        w_start(i, 4 * k + XP, mine, dev(x=xl))

    def ring_relay(i, k):
        low, high = LOW[i], COLS[i] - LOW[i]
        w_wait(i, 4 * k + XM, region(i, xl, side(k), c))
        w_start(i, 4 * k + X2L, region(i, xl, side(k), c, 0, low), dev(x=xr))
        w_wait(i, 4 * k + XP, region(i, xr, side(k), c))
        w_start(i, 4 * k + X2R, region(i, xr, side(k), c, low, high), dev(x=xl))

    def ring_end(i, k):
        low, high = LOW[i], COLS[i] - LOW[i]
        w_wait(i, 4 * k + X2L, region(i, xo, side(k), c, 0, low))
        w_wait(i, 4 * k + X2R, region(i, xo, side(k), c, low, high))
        w_start(i, DC + k, bufs[i].at[:, side(k), c], dev(c=1 - c))

    def sibling_wait(i, k):
        w_wait(i, DC + k, bufs[i].at[:, side(k), 1 - c])

    def cut(i, which):
        size = LOW[i]
        return pl.multiple_of(which * size, 128), size

    def class_start(i):
        lo, size = cut(i, y % 2)
        w_start(i, ZC, region(i, x, zh, c, lo, size), dev(zh=1 - zh))

    def class_swap(i):
        lo, size = cut(i, y % 2)
        w_wait(i, ZC, region(i, x, 1 - zh, c, lo, size))
        w_start(i, YC, region(i, x, 1 - zh, c, lo, size), dev(y=ypair))

    def class_ring(i):
        lo, size = cut(i, 1 - y % 2)
        w_wait(i, YC, region(i, x, 1 - zh, c, lo, size))
        ring_start(i, 1)

    def uneven(which, j):
        lo, size = (0, LOW[0]) if which == 0 else (LOW[0], COLS[0] - LOW[0])
        if j == ZC:
            return w_copy(0, ZC, region(0, x, zh, c, lo, size), dev(zh=1 - zh))
        return w_copy(0, YC, region(0, x, 1 - zh, c, lo, size), dev(y=ypair))

    def by_parity(act):
        for which in (0, 1):

            @pl.when(y % 2 == which)
            def _():
                act(which)

    def first_start():
        by_parity(lambda which: uneven(which, ZC).start())

    def first_swap():
        def act(which):
            uneven(which, ZC).wait_recv()
            uneven(which, YC).start()

        by_parity(act)

    def first_ring():
        by_parity(lambda which: uneven(1 - which, YC).wait_recv())
        ring_start(0, 1)

    def first_sent():
        def act(which):
            uneven(which, ZC).wait_send()
            uneven(which, YC).wait_send()

        by_parity(act)

    loads[0].wait()
    first_start()
    ring_start(0, 0)

    def norm_rows(rows, gain, shift):
        average = jnp.mean(rows, axis=-1, keepdims=True)
        centered = rows - average
        spread = jnp.mean(centered * centered, axis=-1, keepdims=True)
        return centered * lax.rsqrt(spread + EPSILON) * gain[...] + shift[...]

    def norm_image(image, store):
        @pl.loop(0, TOK // 48)
        def _(n):
            at = pl.ds(pl.multiple_of(n * 48, 16), 48)
            rows = x_ref[image, at, :].astype(F32)
            store(at, norm_rows(rows, pre_gain, pre_shift).astype(BF16))

    def store_other(at, value):
        other[at, :] = value

    def store_own(at, value):
        tok[zl, at, :] = value

    def t_copy(src, slot, j, target):
        return pltpu.make_async_remote_copy(
            src_ref=src, dst_ref=tok.at[slot], send_sem=t_send.at[j], recv_sem=t_recv.at[slot],
            device_id=target, device_id_type=MESH,
        )

    norm_image(1 - half, store_other)
    to_near = t_copy(other, zl, 1, dev(zl=near_other))
    to_near.start()
    to_far = t_copy(other, zl, 2, dev(zl=far_other))

    @pl.when(is_near)
    def _():
        to_far.start()

    norm_image(half, store_own)
    to_partner = t_copy(tok.at[zl], zl, 0, dev(zl=partner))
    to_partner.start()

    for load in loads[1:]:
        load.wait()

    onward = t_copy(tok.at[far_other], far_other, 3, dev(zl=partner))

    def token_wait(slot):
        t_copy(tok.at[slot], slot, 0, dev(zl=partner)).wait_recv()

    first_swap()
    ring_relay(0, 0)
    first_ring()
    ring_end(0, 0)
    ring_relay(0, 1)
    for i in (1, 2, 3):
        ring_start(i, 0)

    @pl.when(is_near)
    def _():
        token_wait(far_other)
        onward.start()

    ring_end(0, 1)
    sibling_wait(0, 0)
    sibling_wait(0, 1)

    def slot_of(j):
        last = jnp.where(j == 2, near_other, far_other)
        return jnp.where(j == 0, zl, jnp.where(j == 1, partner, last))

    def y_copy(r, head, slot):
        to = (y + r) % 4
        return pltpu.make_async_remote_copy(
            src_ref=qsend.at[head, to, slot], dst_ref=qin.at[head, y, slot],
            send_sem=y_send.at[head, r - 1, slot], recv_sem=y_recv.at[head, r - 1, slot],
            device_id=dev(y=to), device_id_type=MESH,
        )

    def y_copy_in(r, head, slot, source):
        return pltpu.make_async_remote_copy(
            src_ref=qin.at[head, source, slot], dst_ref=qin.at[head, source, slot],
            send_sem=y_send.at[head, r - 1, slot], recv_sem=y_recv.at[head, r - 1, slot],
            device_id=dev(y=(y + 1) % 4), device_id_type=MESH,
        )

    @pl.loop(0, 4)
    def _(j):
        slot = slot_of(j)

        @pl.when((j > 0) & jnp.logical_not((j == 3) & is_near))
        def _():
            token_wait(slot)

        rows = tok[slot]
        bias_at = pl.multiple_of(part * HALF, 128)
        for n in range(3):
            at = slice(640 * n, 640 * n + 640)
            block = wqkv[:, :, :, :, at].reshape(D, 640)
            bias = qkv_bias[:, pl.ds(bias_at + 640 * n, 640)]
            packed[:, at] = jnp.dot(rows, block, preferred_element_type=F32) + bias
        for head in range(2):
            for to in range(4):
                first = PAIR * to + 240 * head
                start = first // 128 * 128
                wide = packed[:, start : min(start + 384, HALF)]
                shift = first - start
                if shift:
                    wide = pltpu.roll(wide, wide.shape[1] - shift, 1)
                qsend[head, to, slot] = wide[:, :256].astype(BF16)
            qin[head, y, slot] = qsend[head, y, slot]
        for r in (2, 1, 3):
            y_copy(r, 0, slot).start()

    @pl.loop(0, 4)
    def _(j):
        for r in (2, 1, 3):
            y_copy(r, 1, slot_of(j)).start()

    for i in (1, 2, 3):
        class_start(i)
    for i in (1, 2):
        ring_relay(i, 0)

    lane128 = lax.broadcasted_iota(jnp.int32, (TOK, 128), 1)

    def unpack(head):
        @pl.loop(0, 16)
        def _(n):
            j, r = n // 4, n % 4
            slot = slot_of(j)
            source = (y + 4 - r) % 4

            @pl.when(r > 0)
            def _():
                y_copy_in(r, head, slot, source).wait_recv()

            wide = qin[head, source, slot].astype(F32)
            at = pl.ds(pl.multiple_of((source * 4 + slot) * TOK, 16), TOK)
            keep = lane128 < HEAD_DIM
            keys = pltpu.roll(wide, 256 - 80, 1)[:, :128]
            values = pltpu.roll(wide, 256 - 160, 1)[:, :128]
            ones = jnp.where(lane128 == HEAD_DIM, 1.0, 0.0)
            qb[head, at, :] = jnp.where(keep, wide[:, :128], 0.0).astype(BF16)
            kb[head, at, :] = jnp.where(keep, keys, 0.0).astype(BF16)
            vb[head, at, :] = jnp.where(keep, values, ones).astype(BF16)

    order = (2, 1, 3, 0)

    def c_copy(head, t):
        to = (y + order[t]) % 4
        return pltpu.make_async_remote_copy(
            src_ref=csend.at[head, to], dst_ref=cin.at[head, y],
            send_sem=c_send.at[head, t], recv_sem=c_recv.at[head, t],
            device_id=dev(y=to), device_id_type=MESH,
        )

    def c_wait(head, t):
        source = (y + 4 - order[t]) % 4
        pltpu.make_async_remote_copy(
            src_ref=cin.at[head, source], dst_ref=cin.at[head, source],
            send_sem=c_send.at[head, t], recv_sem=c_recv.at[head, t],
            device_id=dev(y=(y + 1) % 4), device_id_type=MESH,
        ).wait_recv()

    wide_lane = lax.broadcasted_iota(jnp.int32, (4 * TOK, 128), 1)

    def score(head, t, scores):
        to = (y + order[t]) % 4
        at = pl.ds(pl.multiple_of(to * 4 * TOK, 16), 4 * TOK)
        scores[...] = lax.dot_general(
            qb[head, at, :], kb[head], (((1,), (1,)), ((), ())), preferred_element_type=F32
        )

    def mix(head, t, scores):
        to = (y + order[t]) % 4
        highest = jnp.max(scores[...], axis=-1, keepdims=True) * EXP_SCALE
        weights = jnp.exp2(scores[...] * EXP_SCALE - highest).astype(BF16)
        total = jnp.dot(weights, vb[head], preferred_element_type=F32)
        mixed = jnp.where(wide_lane < HEAD_DIM, total / total[:, HEAD_DIM : HEAD_DIM + 1], 0.0)
        csend[head, to] = mixed.astype(BF16)

    def attend(head):
        slots = (score_a, score_b)
        score(head, 0, slots[0])
        for t in range(4):
            if t < 3:
                score(head, t + 1, slots[(t + 1) % 2])
            mix(head, t, slots[t % 2])
            if t < 3:
                c_copy(head, t).start()
        cin[head, y] = csend[head, y]

    def z_place(of_half, of_part):
        return of_half, pl.ds(pl.multiple_of(384 * of_part, 128), 384)

    def z_copy(head, d):
        at_half, at = z_place(half, part)
        return pltpu.make_async_remote_copy(
            src_ref=zsend.at[head, d], dst_ref=ctx.at[head, at_half, :, at],
            send_sem=z_send.at[head, d], recv_sem=z_recv.at[head, d],
            device_id=dev(zl=(zl + d) % 4), device_id_type=MESH,
        )

    def z_wait(head):
        for d in (1, 2, 3):
            source = (zl + 4 - d) % 4
            at_half, at = z_place(source // 2, source % 2)
            ref = ctx.at[head, at_half, :, at]
            pltpu.make_async_remote_copy(
                src_ref=ref, dst_ref=ref, send_sem=z_send.at[head, d], recv_sem=z_recv.at[head, d],
                device_id=dev(zl=partner), device_id_type=MESH,
            ).wait_recv()

    def give_back(head):
        for t in range(3):
            c_wait(head, t)
        for d in (2, 3, 1, 0):
            to = (zl + d) % 4
            at = pl.ds(pl.multiple_of(to * TOK, 16), TOK)
            joined = None
            for s in range(4):
                piece = cin[head, s, at, :].astype(F32)
                wide = jnp.concatenate([piece, jnp.zeros((TOK, 256), F32)], axis=1)
                if s:
                    wide = pltpu.roll(wide, 80 * s, 1)
                joined = wide if joined is None else joined + wide
            if d:
                zsend[head, d] = joined.astype(BF16)
                z_copy(head, d).start()
            else:
                at_half, at = z_place(half, part)
                ctx[head, at_half, :, at] = joined.astype(BF16)

    rows = 2 * TOK

    def project(head):
        @pl.loop(0, 5)
        def _(n):
            at = pl.ds(pl.multiple_of(256 * n, 256), 256)
            made = None
            for p in range(2):
                block = wout[2 * p : 2 * p + 2, :, head, :, at].reshape(320, 256)
                left = ctx[head, :, :, 384 * p : 384 * p + 320].reshape(rows, 320)
                term = jnp.dot(left, block, preferred_element_type=F32)
                made = term if made is None else made + term
            if head == 0:
                mid[:, at] = x_ref[:, :, at].reshape(rows, 256).astype(F32) + made + out_bias[:, at]
            else:
                mid[:, at] += made

    unpack(0)
    ring_relay(3, 0)
    attend(0)
    for i in (1, 2, 3):
        ring_end(i, 0)
    class_swap(1)
    class_swap(2)
    give_back(0)
    unpack(1)
    class_ring(1)
    class_ring(2)
    class_swap(3)
    attend(1)
    class_ring(3)
    give_back(1)
    ring_relay(1, 1)
    ring_relay(2, 1)
    ring_relay(3, 1)
    ring_end(1, 1)
    sibling_wait(1, 0)
    sibling_wait(1, 1)
    z_wait(0)
    project(0)
    ring_end(2, 1)
    z_wait(1)
    project(1)

    @pl.loop(0, rows // 48)
    def _(n):
        at = pl.ds(pl.multiple_of(n * 48, 16), 48)
        normed_mlp[at, :] = norm_rows(mid[at, :], mlp_gain, mlp_shift).astype(BF16)

    ring_end(3, 1)
    sibling_wait(2, 0)
    sibling_wait(2, 1)

    @pl.loop(0, 10)
    def _(n):
        at = pl.ds(pl.multiple_of(256 * n, 256), 256)
        block = wup[:, :, :, :, at].reshape(D, 256)
        lifted = jnp.dot(normed_mlp[...], block, preferred_element_type=F32) + up_bias[:, at]
        hid[:, at] = (0.5 * lifted * (1.0 + lax.erf(lifted * math.sqrt(0.5)))).astype(BF16)

    sibling_wait(3, 0)
    sibling_wait(3, 1)

    @pl.loop(0, 5)
    def _(n):
        at = pl.ds(pl.multiple_of(256 * n, 256), 256)
        block = wdown[:, :, :, :, at].reshape(FF, 256)
        lowered = jnp.dot(hid[...], block, preferred_element_type=F32)
        result = mid[:, at] + lowered + down_bias[:, at]
        o_ref[:, :, at] = result.astype(BF16).reshape(2, TOK, 256)

    for copy in started:
        copy.wait_send()
    to_partner.wait_send()
    to_near.wait_send()

    @pl.when(is_near)
    def _():
        to_far.wait_send()
        onward.wait_send()

    @pl.loop(0, 4)
    def _(slot):
        for head in range(2):
            for r in (1, 2, 3):
                y_copy(r, head, slot).wait_send()

    for head in range(2):
        for t in range(3):
            c_copy(head, t).wait_send()
        for d in (1, 2, 3):
            z_copy(head, d).wait_send()
    first_sent()


def layer(
    tokens, pre_gain, pre_shift, w_qkv, qkv_bias, w_out, out_bias,
    mlp_gain, mlp_shift, w_up, up_bias, w_down, down_bias,
):
    vmem = pl.BlockSpec(memory_space=pltpu.VMEM)
    hbm = pl.BlockSpec(memory_space=pltpu.HBM)
    dma = pltpu.SemaphoreType.DMA
    vectors = (pre_gain, pre_shift, qkv_bias, out_bias, mlp_gain, mlp_shift, up_bias, down_bias)
    rows = [vector[None] for vector in vectors]
    return pl.pallas_call(
        kernel,
        out_shape=jax.ShapeDtypeStruct((2, TOK, D), BF16),
        in_specs=[vmem] * 9 + [hbm] * 4,
        out_specs=vmem,
        scratch_shapes=[
            pltpu.VMEM((4, 2, 2, 80, HALF), BF16),
            pltpu.VMEM((4, 2, 2, 80, D), BF16),
            pltpu.VMEM((4, 2, 2, 80, FF), BF16),
            pltpu.VMEM((4, 2, 2, 160, D), BF16),
            pltpu.VMEM((4, TOK, D), BF16),
            pltpu.VMEM((TOK, D), BF16),
            pltpu.VMEM((TOK, HALF), F32),
            pltpu.VMEM((2, 4, 4, TOK, 256), BF16),
            pltpu.VMEM((2, 4, 4, TOK, 256), BF16),
            pltpu.VMEM((2, SEQ, 128), BF16),
            pltpu.VMEM((2, SEQ, 128), BF16),
            pltpu.VMEM((2, SEQ, 128), BF16),
            pltpu.VMEM((4 * TOK, SEQ), F32),
            pltpu.VMEM((4 * TOK, SEQ), F32),
            pltpu.VMEM((2, 4, 4 * TOK, 128), BF16),
            pltpu.VMEM((2, 4, 4 * TOK, 128), BF16),
            pltpu.VMEM((2, 4, TOK, 384), BF16),
            pltpu.VMEM((2, 2, TOK, 768), BF16),
            pltpu.VMEM((2 * TOK, D), F32),
            pltpu.VMEM((2 * TOK, D), BF16),
            pltpu.VMEM((2 * TOK, FF), BF16),
            dma((4,)), dma((4, 12)), dma((4, 12)), dma((4,)), dma((4,)),
            dma((2, 3, 4)), dma((2, 3, 4)), dma((2, 3)), dma((2, 3)), dma((2, 4)), dma((2, 4)),
        ],
        compiler_params=pltpu.CompilerParams(
            collective_id=0, has_side_effects=True, vmem_limit_bytes=67043328
        ),
    )(
        tokens, *rows,
        w_qkv, w_out, w_up, w_down,
    )


def solution(mesh):
    in_specs = (
        P("dp", "seq", None),
        P(), P(), P("dp", None), P(), P("dp", None), P(), P(), P(), P("dp", None), P(),
        P("dp", None), P(),
    )
    out_specs = P("dp", "seq", None)
    return jax.shard_map(layer, mesh=mesh, in_specs=in_specs, out_specs=out_specs, check_vma=False)
```

time: 164 us -> 133 us (0.81)
  the two profiles are of different devices: /device:TPU:33 before, /device:TPU:1 now
where the time goes in v2:
time: 133 us
  Pallas kernels  125 us (94%)
  local copies, waits for them, and re-layouts  7.84 us (6%)
    pallas_call x1, Pallas kernels, layer(): pl.pallas_call(kernel, out_shape=jax.ShapeDtypeStruct((2, TOK, D), BF16),...  125 us
    broadcast_in_dim x8, local copies, waits for them, and re-layouts, layer(): rows = [vector[None] for vector in vectors]  5.48 us

profile of v2, /device:TPU:1, one launch (start us, length us, event | category | flops | bytes accessed | tf_op | source)
XLA Modules:
  0.0 133.0 jit_solution(17939738578264678633)
XLA Ops:
  0.0 0.0 copy-start.2
  0.0 1.3 broadcast_in_dim.24.pre_gain
  1.3 0.0 copy-done.2
  1.3 0.0 copy-start.3
  1.3 0.6 broadcast_in_dim.25.pre_shift
  1.9 0.1 copy-done.3
  2.0 0.0 copy-start.4
  2.0 0.6 broadcast_in_dim.27.out_bias
  2.6 0.1 copy-done.4
  2.7 0.0 copy-start.5
  2.7 0.0 copy-start.6
  2.7 0.6 broadcast_in_dim.28.mlp_gain
  3.3 0.1 copy-done.5
  3.4 0.0 copy-start.1
  3.4 0.6 broadcast_in_dim.29.mlp_shift
  4.0 0.0 copy-done.6
  4.0 0.0 copy-start
  4.0 0.6 broadcast_in_dim.31.down_bias
  4.6 0.0 copy-done.1
  4.6 0.6 broadcast_in_dim.30.up_bias
  5.2 0.0 copy-done
  5.2 0.6 broadcast_in_dim.26.qkv_bias
  5.8 125.1 %shard_map.127 = bf16[2,144,1280]{2,1,0:T(8,128)(2,1)} custom-call(bf16[2,144,1280]{2,1,0:T(8,128)(2,1)} %x_ref.1, f32[1,1280]{1,0:T(1,128)} %broadcast_in_dim.24.pre_gain, f32[1,1280]{1,0:T(1,128)} %broadcast_in_dim.25.pre_shift, f32[1,3840]{1,0:T(1,128)} %broadcast_in_dim.26.qkv_bias, f32[1,1280]{1,0:T(1,128)} %broadcast_in_dim.27.out_bias, ...), custom_call_target="tpu_custom_call" | custom-call | tf_op jit(solution)/shard_map/pallas_call | solution.py:511
  131.0 2.0 %copy.15 = bf16[2,144,1280]{2,1,0:T(8,128)(2,1)} copy(bf16[2,144,1280]{2,1,0:T(8,128)(2,1)} %shard_map.127) | data formatting | bytes 1474560
Async XLA Ops:
  0.0 1.3 copy-start.2
  1.3 0.7 copy-start.3
  2.0 0.7 copy-start.4
  2.7 0.7 copy-start.5
  2.7 1.3 copy-start.6
  3.4 1.2 copy-start.1
  4.0 1.2 copy-start

commit v3 on v2

--- a/solution.py
+++ b/solution.py
@@ -25,7 +25,7 @@
 COLS = (HALF, D, FF, D)
 LOW = (1024, 640, 1280, 640)
 ROWS = (80, 80, 80, 160)
-XM, XP, X2L, X2R, ZC, YC, DC = 0, 1, 2, 3, 8, 9, 10
+XM, XP, X2L, X2R, ZC, YC, YQ, DC = 0, 1, 2, 3, 8, 9, 10, 13
 
 
 def kernel(
@@ -97,43 +97,60 @@
     def side(k):
         return zh if k == 0 else 1 - zh
 
+    def to_sibling(i, k, n, xx):
+        w_start(i, DC + 4 * k + n, region(i, xx, side(k), c), dev(c=1 - c))
+
     def ring_start(i, k):
         mine = region(i, x, side(k), c)
         w_start(i, 4 * k + XM, mine, dev(x=xr))
         w_start(i, 4 * k + XP, mine, dev(x=xl))
+        to_sibling(i, k, 0, x)
 
     def ring_relay(i, k):
         low, high = LOW[i], COLS[i] - LOW[i]
         w_wait(i, 4 * k + XM, region(i, xl, side(k), c))
         w_start(i, 4 * k + X2L, region(i, xl, side(k), c, 0, low), dev(x=xr))
+        to_sibling(i, k, 1, xl)
         w_wait(i, 4 * k + XP, region(i, xr, side(k), c))
         w_start(i, 4 * k + X2R, region(i, xr, side(k), c, low, high), dev(x=xl))
+        to_sibling(i, k, 2, xr)
 
     def ring_end(i, k):
         low, high = LOW[i], COLS[i] - LOW[i]
         w_wait(i, 4 * k + X2L, region(i, xo, side(k), c, 0, low))
         w_wait(i, 4 * k + X2R, region(i, xo, side(k), c, low, high))
-        w_start(i, DC + k, bufs[i].at[:, side(k), c], dev(c=1 - c))
+        to_sibling(i, k, 3, xo)
 
     def sibling_wait(i, k):
-        w_wait(i, DC + k, bufs[i].at[:, side(k), 1 - c])
-
-    def cut(i, which):
-        size = LOW[i]
-        return pl.multiple_of(which * size, 128), size
+        for n, xx in enumerate((x, xl, xr, xo)):
+            w_wait(i, DC + 4 * k + n, region(i, xx, side(k), 1 - c))
+
+    def piece(i, zz, who):
+        if i == 1:
+            return region(i, x, zz, c, pl.multiple_of(640 * (who % 2), 128), 640)
+        if i == 2:
+            return region(i, x, zz, c, pl.multiple_of(640 * who, 128), 640)
+        down = pl.ds(pl.multiple_of(80 * (who // 2), 16), 80)
+        return bufs[i].at[x, zz, c, down, pl.ds(pl.multiple_of(640 * (who % 2), 128), 640)]
 
     def class_start(i):
-        lo, size = cut(i, y % 2)
-        w_start(i, ZC, region(i, x, zh, c, lo, size), dev(zh=1 - zh))
+        w_start(i, ZC, piece(i, zh, y), dev(zh=1 - zh))
 
     def class_swap(i):
-        lo, size = cut(i, y % 2)
-        w_wait(i, ZC, region(i, x, 1 - zh, c, lo, size))
-        w_start(i, YC, region(i, x, 1 - zh, c, lo, size), dev(y=ypair))
+        mine = piece(i, 1 - zh, y)
+        w_wait(i, ZC, mine)
+        if i == 1:
+            w_start(i, YQ, mine, dev(y=ypair))
+        else:
+            for r in (2, 1, 3):
+                w_start(i, YQ + r - 1, mine, dev(y=(y + r) % 4))
 
     def class_ring(i):
-        lo, size = cut(i, 1 - y % 2)
-        w_wait(i, YC, region(i, x, 1 - zh, c, lo, size))
+        if i == 1:
+            w_wait(i, YQ, piece(i, 1 - zh, ypair))
+        else:
+            for r in (1, 2, 3):
+                w_wait(i, YQ + r - 1, piece(i, 1 - zh, (y + 4 - r) % 4))
         ring_start(i, 1)
 
     def uneven(which, j):
@@ -174,11 +191,14 @@
     first_start()
     ring_start(0, 0)
 
+    def row_of(ref, at=slice(None)):
+        return ref[at].reshape(1, -1)
+
     def norm_rows(rows, gain, shift):
         average = jnp.mean(rows, axis=-1, keepdims=True)
         centered = rows - average
         spread = jnp.mean(centered * centered, axis=-1, keepdims=True)
-        return centered * lax.rsqrt(spread + EPSILON) * gain[...] + shift[...]
+        return centered * lax.rsqrt(spread + EPSILON) * row_of(gain) + row_of(shift)
 
     def norm_image(image, store):
         @pl.loop(0, TOK // 48)
@@ -214,6 +234,7 @@
 
     for load in loads[1:]:
         load.wait()
+    class_start(1)
 
     onward = t_copy(tok.at[far_other], far_other, 3, dev(zl=partner))
 
@@ -234,6 +255,7 @@
         onward.start()
 
     ring_end(0, 1)
+    class_swap(1)
     sibling_wait(0, 0)
     sibling_wait(0, 1)
 
@@ -256,8 +278,7 @@
             device_id=dev(y=(y + 1) % 4), device_id_type=MESH,
         )
 
-    @pl.loop(0, 4)
-    def _(j):
+    def first_projection(j):
         slot = slot_of(j)
 
         @pl.when((j > 0) & jnp.logical_not((j == 3) & is_near))
@@ -269,7 +290,7 @@
         for n in range(3):
             at = slice(640 * n, 640 * n + 640)
             block = wqkv[:, :, :, :, at].reshape(D, 640)
-            bias = qkv_bias[:, pl.ds(bias_at + 640 * n, 640)]
+            bias = row_of(qkv_bias, pl.ds(bias_at + 640 * n, 640))
             packed[:, at] = jnp.dot(rows, block, preferred_element_type=F32) + bias
         for head in range(2):
             for to in range(4):
@@ -284,15 +305,18 @@
         for r in (2, 1, 3):
             y_copy(r, 0, slot).start()
 
+    pl.loop(0, 4)(first_projection)
+
     @pl.loop(0, 4)
     def _(j):
         for r in (2, 1, 3):
             y_copy(r, 1, slot_of(j)).start()
 
-    for i in (1, 2, 3):
-        class_start(i)
+    class_start(2)
+    class_start(3)
     for i in (1, 2):
         ring_relay(i, 0)
+    class_ring(1)
 
     lane128 = lax.broadcasted_iota(jnp.int32, (TOK, 128), 1)
 
@@ -352,7 +376,7 @@
         mixed = jnp.where(wide_lane < HEAD_DIM, total / total[:, HEAD_DIM : HEAD_DIM + 1], 0.0)
         csend[head, to] = mixed.astype(BF16)
 
-    def attend(head):
+    def attend(head, between):
         slots = (score_a, score_b)
         score(head, 0, slots[0])
         for t in range(4):
@@ -361,6 +385,8 @@
             mix(head, t, slots[t % 2])
             if t < 3:
                 c_copy(head, t).start()
+            if t in between:
+                between[t]()
         cin[head, y] = csend[head, y]
 
     def z_place(of_half, of_part):
@@ -417,43 +443,38 @@
                 term = jnp.dot(left, block, preferred_element_type=F32)
                 made = term if made is None else made + term
             if head == 0:
-                mid[:, at] = x_ref[:, :, at].reshape(rows, 256).astype(F32) + made + out_bias[:, at]
+                mid[:, at] = x_ref[:, :, at].reshape(rows, 256).astype(F32) + made + row_of(out_bias, at)
             else:
                 mid[:, at] += made
 
     unpack(0)
+    class_swap(2)
     ring_relay(3, 0)
-    attend(0)
-    for i in (1, 2, 3):
-        ring_end(i, 0)
-    class_swap(1)
-    class_swap(2)
+    attend(0, {1: lambda: ring_end(1, 0), 2: lambda: ring_end(2, 0)})
+    ring_relay(1, 1)
+    class_swap(3)
+    unpack(1)
+    attend(1, {1: lambda: class_ring(2)})
     give_back(0)
-    unpack(1)
-    class_ring(1)
-    class_ring(2)
-    class_swap(3)
-    attend(1)
     class_ring(3)
     give_back(1)
-    ring_relay(1, 1)
     ring_relay(2, 1)
-    ring_relay(3, 1)
+    ring_end(3, 0)
     ring_end(1, 1)
     sibling_wait(1, 0)
     sibling_wait(1, 1)
     z_wait(0)
     project(0)
-    ring_end(2, 1)
     z_wait(1)
     project(1)
+    ring_relay(3, 1)
+    ring_end(2, 1)
 
     @pl.loop(0, rows // 48)
     def _(n):
         at = pl.ds(pl.multiple_of(n * 48, 16), 48)
         normed_mlp[at, :] = norm_rows(mid[at, :], mlp_gain, mlp_shift).astype(BF16)
 
-    ring_end(3, 1)
     sibling_wait(2, 0)
     sibling_wait(2, 1)
 
@@ -461,9 +482,10 @@
     def _(n):
         at = pl.ds(pl.multiple_of(256 * n, 256), 256)
         block = wup[:, :, :, :, at].reshape(D, 256)
-        lifted = jnp.dot(normed_mlp[...], block, preferred_element_type=F32) + up_bias[:, at]
+        lifted = jnp.dot(normed_mlp[...], block, preferred_element_type=F32) + row_of(up_bias, at)
         hid[:, at] = (0.5 * lifted * (1.0 + lax.erf(lifted * math.sqrt(0.5)))).astype(BF16)
 
+    ring_end(3, 1)
     sibling_wait(3, 0)
     sibling_wait(3, 1)
 
@@ -472,7 +494,7 @@
         at = pl.ds(pl.multiple_of(256 * n, 256), 256)
         block = wdown[:, :, :, :, at].reshape(FF, 256)
         lowered = jnp.dot(hid[...], block, preferred_element_type=F32)
-        result = mid[:, at] + lowered + down_bias[:, at]
+        result = mid[:, at] + lowered + row_of(down_bias, at)
         o_ref[:, :, at] = result.astype(BF16).reshape(2, TOK, 256)
 
     for copy in started:
@@ -507,7 +529,6 @@
     hbm = pl.BlockSpec(memory_space=pltpu.HBM)
     dma = pltpu.SemaphoreType.DMA
     vectors = (pre_gain, pre_shift, qkv_bias, out_bias, mlp_gain, mlp_shift, up_bias, down_bias)
-    rows = [vector[None] for vector in vectors]
     return pl.pallas_call(
         kernel,
         out_shape=jax.ShapeDtypeStruct((2, TOK, D), BF16),
@@ -535,14 +556,14 @@
             pltpu.VMEM((2 * TOK, D), F32),
             pltpu.VMEM((2 * TOK, D), BF16),
             pltpu.VMEM((2 * TOK, FF), BF16),
-            dma((4,)), dma((4, 12)), dma((4, 12)), dma((4,)), dma((4,)),
+            dma((4,)), dma((4, 21)), dma((4, 21)), dma((4,)), dma((4,)),
             dma((2, 3, 4)), dma((2, 3, 4)), dma((2, 3)), dma((2, 3)), dma((2, 4)), dma((2, 4)),
         ],
         compiler_params=pltpu.CompilerParams(
             collective_id=0, has_side_effects=True, vmem_limit_bytes=67043328
         ),
     )(
-        tokens, *rows,
+        tokens, *vectors,
         w_qkv, w_out, w_up, w_down,
     )
 

time: 133 us -> 120 us (0.902)
  Pallas kernels: 125 us -> 118 us
  local copies, waits for them, and re-layouts: 7.84 us -> 2.03 us
    pallas_call x1, Pallas kernels: 125 us -> 118 us  [layer(): pl.pallas_call(kernel, out_shape=jax.ShapeDtypeStruct((2, TOK, D), BF16),...]
    broadcast_in_dim x8 -> x0, local copies, waits for them, and re-layouts: 5.48 us -> none  [layer(): rows = [vector[None] for vector in vectors]]
where the time goes in v3:
time: 120 us
  Pallas kernels  118 us (98%)
  local copies, waits for them, and re-layouts  2.03 us (2%)
    pallas_call x1, Pallas kernels, layer(): pl.pallas_call(kernel, out_shape=jax.ShapeDtypeStruct((2, TOK, D), BF16),...  118 us

profile of v3, /device:TPU:1, one launch (start us, length us, event | category | flops | bytes accessed | tf_op | source)
XLA Modules:
  0.0 119.7 jit_solution(7150587744575314793)
XLA Ops:
  0.0 117.7 %shard_map.127 = bf16[2,144,1280]{2,1,0:T(8,128)(2,1)} custom-call(bf16[2,144,1280]{2,1,0:T(8,128)(2,1)} %x_ref.1, f32[1280]{0:T(1024)} %pre_gain.1, f32[1280]{0:T(1024)} %pre_shift.1, f32[3840]{0:T(1024)} %qkv_bias.1, f32[1280]{0:T(1024)} %out_bias.1, f32[1280]{0:T(1024)} %mlp_gain.1, f32[1280]{0:T(1024)} %mlp_shift.1, f32[2560]{0:T(1024)} %up_bias.1, ...), custom_call_target="tpu_custom_call" | custom-call | tf_op jit(solution)/shard_map/pallas_call | solution.py:532
  117.7 2.0 %copy.15 = bf16[2,144,1280]{2,1,0:T(8,128)(2,1)} copy(bf16[2,144,1280]{2,1,0:T(8,128)(2,1)} %shard_map.127) | data formatting | bytes 1474560

commit v4 on v3

--- a/solution.py
+++ b/solution.py
@@ -29,9 +29,11 @@
 
 
 def kernel(
-    x_ref, pre_gain, pre_shift, qkv_bias, out_bias, mlp_gain, mlp_shift, up_bias, down_bias,
+    x_in, pre_gain_in, pre_shift_in, qkv_bias_in, out_bias_in, mlp_gain_in, mlp_shift_in,
+    up_bias_in, down_bias_in,
     wqkv_in, wout_in, wup_in, wdown_in,
     o_ref,
+    x_ref, pre_gain, pre_shift, qkv_bias, out_bias, mlp_gain, mlp_shift, up_bias, down_bias,
     wqkv, wout, wup, wdown,
     tok, other, packed, qsend, qin, qb, kb, vb, score_a, score_b, csend, cin, zsend, ctx, mid, normed_mlp, hid,
     load_sem, w_send, w_recv, t_send, t_recv, y_send, y_recv, c_send, c_recv, z_send, z_recv,
@@ -68,11 +70,22 @@
     loads = [
         pltpu.make_async_copy(sources[i], bufs[i].at[x, zh, c], load_sem.at[i]) for i in range(4)
     ]
-    for load in loads:
-        load.start()
+    early_in = (x_in, pre_gain_in, pre_shift_in)
+    late_in = (qkv_bias_in, out_bias_in, mlp_gain_in, mlp_shift_in, up_bias_in, down_bias_in)
+    early_to = (x_ref, pre_gain, pre_shift)
+    late_to = (qkv_bias, out_bias, mlp_gain, mlp_shift, up_bias, down_bias)
+    early = [
+        pltpu.make_async_copy(a, b, load_sem.at[4 + n])
+        for n, (a, b) in enumerate(zip(early_in, early_to))
+    ]
+    late = [
+        pltpu.make_async_copy(a, b, load_sem.at[7 + n])
+        for n, (a, b) in enumerate(zip(late_in, late_to))
+    ]
     for peer in peers:
         pl.semaphore_signal(barrier, inc=1, device_id=peer, device_id_type=MESH)
-    pl.semaphore_wait(barrier, len(peers))
+    for load in (loads[0], *early, *loads[1:], *late):
+        load.start()
 
     started = []
 
@@ -187,10 +200,6 @@
 
         by_parity(act)
 
-    loads[0].wait()
-    first_start()
-    ring_start(0, 0)
-
     def row_of(ref, at=slice(None)):
         return ref[at].reshape(1, -1)
 
@@ -219,7 +228,15 @@
             device_id=target, device_id_type=MESH,
         )
 
+    for load in early:
+        load.wait()
     norm_image(1 - half, store_other)
+    norm_image(half, store_own)
+    loads[0].wait()
+    pl.semaphore_wait(barrier, len(peers))
+
+    first_start()
+    ring_start(0, 0)
     to_near = t_copy(other, zl, 1, dev(zl=near_other))
     to_near.start()
     to_far = t_copy(other, zl, 2, dev(zl=far_other))
@@ -228,11 +245,10 @@
     def _():
         to_far.start()
 
-    norm_image(half, store_own)
     to_partner = t_copy(tok.at[zl], zl, 0, dev(zl=partner))
     to_partner.start()
 
-    for load in loads[1:]:
+    for load in (*loads[1:], *late):
         load.wait()
     class_start(1)
 
@@ -433,7 +449,7 @@
     rows = 2 * TOK
 
     def project(head):
-        @pl.loop(0, 5)
+        @pl.loop(0, 5, unroll=True)
         def _(n):
             at = pl.ds(pl.multiple_of(256 * n, 256), 256)
             made = None
@@ -478,7 +494,7 @@
     sibling_wait(2, 0)
     sibling_wait(2, 1)
 
-    @pl.loop(0, 10)
+    @pl.loop(0, 10, unroll=2)
     def _(n):
         at = pl.ds(pl.multiple_of(256 * n, 256), 256)
         block = wup[:, :, :, :, at].reshape(D, 256)
@@ -489,7 +505,7 @@
     sibling_wait(3, 0)
     sibling_wait(3, 1)
 
-    @pl.loop(0, 5)
+    @pl.loop(0, 5, unroll=True)
     def _(n):
         at = pl.ds(pl.multiple_of(256 * n, 256), 256)
         block = wdown[:, :, :, :, at].reshape(FF, 256)
@@ -532,9 +548,11 @@
     return pl.pallas_call(
         kernel,
         out_shape=jax.ShapeDtypeStruct((2, TOK, D), BF16),
-        in_specs=[vmem] * 9 + [hbm] * 4,
+        in_specs=[hbm] * 13,
         out_specs=vmem,
         scratch_shapes=[
+            pltpu.VMEM((2, TOK, D), BF16),
+            *[pltpu.VMEM(vector.shape, F32) for vector in vectors],
             pltpu.VMEM((4, 2, 2, 80, HALF), BF16),
             pltpu.VMEM((4, 2, 2, 80, D), BF16),
             pltpu.VMEM((4, 2, 2, 80, FF), BF16),
@@ -556,7 +574,7 @@
             pltpu.VMEM((2 * TOK, D), F32),
             pltpu.VMEM((2 * TOK, D), BF16),
             pltpu.VMEM((2 * TOK, FF), BF16),
-            dma((4,)), dma((4, 21)), dma((4, 21)), dma((4,)), dma((4,)),
+            dma((13,)), dma((4, 21)), dma((4, 21)), dma((4,)), dma((4,)),
             dma((2, 3, 4)), dma((2, 3, 4)), dma((2, 3)), dma((2, 3)), dma((2, 4)), dma((2, 4)),
         ],
         compiler_params=pltpu.CompilerParams(

time: 120 us -> 117 us (0.975)
  Pallas kernels: 118 us -> 115 us
    pallas_call x1, Pallas kernels: 118 us -> 115 us  [layer(): pl.pallas_call(kernel, out_shape=jax.ShapeDtypeStruct((2, TOK, D), BF16),...]
where the time goes in v4:
time: 117 us
  Pallas kernels  115 us (98%)
  local copies, waits for them, and re-layouts  2.03 us (2%)
    pallas_call x1, Pallas kernels, layer(): pl.pallas_call(kernel, out_shape=jax.ShapeDtypeStruct((2, TOK, D), BF16),...  115 us

profile of v4, /device:TPU:1, one launch (start us, length us, event | category | flops | bytes accessed | tf_op | source)
XLA Modules:
  0.0 117.1 jit_solution(5375528508495913614)
XLA Ops:
  0.0 115.0 %shard_map.127 = bf16[2,144,1280]{2,1,0:T(8,128)(2,1)} custom-call(bf16[2,144,1280]{2,1,0:T(8,128)(2,1)} %x_in.1, f32[1280]{0:T(1024)} %pre_gain_in.1, f32[1280]{0:T(1024)} %pre_shift_in.1, f32[3840]{0:T(1024)} %qkv_bias_in.1, f32[1280]{0:T(1024)} %out_bias_in.1, f32[1280]{0:T(1024)} %mlp_gain_in.1, f32[1280]{0:T(1024)} %mlp_shift_in.1, f32[2560]{0:T(1024)} %up_bias_in.1, ...), custom_call_target="tpu_custom_call" | custom-call | tf_op jit(solution)/shard_map/pallas_call | solution.py:548
  115.1 2.0 %copy.15 = bf16[2,144,1280]{2,1,0:T(8,128)(2,1)} copy(bf16[2,144,1280]{2,1,0:T(8,128)(2,1)} %shard_map.127) | data formatting | bytes 1474560

commit v5 on v4

--- a/solution.py
+++ b/solution.py
@@ -359,10 +359,13 @@
 
     order = (2, 1, 3, 0)
 
+    def c_place(head, source):
+        return cin.at[head, pl.ds(pl.multiple_of(source * HEAD_DIM, 16), HEAD_DIM), :]
+
     def c_copy(head, t):
         to = (y + order[t]) % 4
         return pltpu.make_async_remote_copy(
-            src_ref=csend.at[head, to], dst_ref=cin.at[head, y],
+            src_ref=csend.at[head, to], dst_ref=c_place(head, y),
             send_sem=c_send.at[head, t], recv_sem=c_recv.at[head, t],
             device_id=dev(y=to), device_id_type=MESH,
         )
@@ -370,12 +373,10 @@
     def c_wait(head, t):
         source = (y + 4 - order[t]) % 4
         pltpu.make_async_remote_copy(
-            src_ref=cin.at[head, source], dst_ref=cin.at[head, source],
+            src_ref=c_place(head, source), dst_ref=c_place(head, source),
             send_sem=c_send.at[head, t], recv_sem=c_recv.at[head, t],
             device_id=dev(y=(y + 1) % 4), device_id_type=MESH,
         ).wait_recv()
-
-    wide_lane = lax.broadcasted_iota(jnp.int32, (4 * TOK, 128), 1)
 
     def score(head, t, scores):
         to = (y + order[t]) % 4
@@ -389,8 +390,9 @@
         highest = jnp.max(scores[...], axis=-1, keepdims=True) * EXP_SCALE
         weights = jnp.exp2(scores[...] * EXP_SCALE - highest).astype(BF16)
         total = jnp.dot(weights, vb[head], preferred_element_type=F32)
-        mixed = jnp.where(wide_lane < HEAD_DIM, total / total[:, HEAD_DIM : HEAD_DIM + 1], 0.0)
-        csend[head, to] = mixed.astype(BF16)
+        mixed = total / total[:, HEAD_DIM : HEAD_DIM + 1]
+        tall = jnp.concatenate([mixed, jnp.zeros((64, 128), F32)], axis=0)
+        csend[head, to] = tall.T[:HEAD_DIM].astype(BF16)
 
     def attend(head, between):
         slots = (score_a, score_b)
@@ -403,15 +405,18 @@
                 c_copy(head, t).start()
             if t in between:
                 between[t]()
-        cin[head, y] = csend[head, y]
+        c_place(head, y)[...] = csend[head, y]
 
     def z_place(of_half, of_part):
         return of_half, pl.ds(pl.multiple_of(384 * of_part, 128), 384)
+
+    def z_rows(head, to):
+        return zsend.at[head, pl.ds(pl.multiple_of(to * TOK, 16), TOK), :]
 
     def z_copy(head, d):
         at_half, at = z_place(half, part)
         return pltpu.make_async_remote_copy(
-            src_ref=zsend.at[head, d], dst_ref=ctx.at[head, at_half, :, at],
+            src_ref=z_rows(head, (zl + d) % 4), dst_ref=ctx.at[head, at_half, :, at],
             send_sem=z_send.at[head, d], recv_sem=z_recv.at[head, d],
             device_id=dev(zl=(zl + d) % 4), device_id_type=MESH,
         )
@@ -429,22 +434,13 @@
     def give_back(head):
         for t in range(3):
             c_wait(head, t)
-        for d in (2, 3, 1, 0):
-            to = (zl + d) % 4
-            at = pl.ds(pl.multiple_of(to * TOK, 16), TOK)
-            joined = None
-            for s in range(4):
-                piece = cin[head, s, at, :].astype(F32)
-                wide = jnp.concatenate([piece, jnp.zeros((TOK, 256), F32)], axis=1)
-                if s:
-                    wide = pltpu.roll(wide, 80 * s, 1)
-                joined = wide if joined is None else joined + wide
-            if d:
-                zsend[head, d] = joined.astype(BF16)
-                z_copy(head, d).start()
-            else:
-                at_half, at = z_place(half, part)
-                ctx[head, at_half, :, at] = joined.astype(BF16)
+        for n in range(5):
+            at = slice(128 * n, 128 * n + 128)
+            zsend[head, at, :] = cin[head, :, at].astype(F32).T.astype(BF16)
+        for d in (2, 3, 1):
+            z_copy(head, d).start()
+        at_half, at = z_place(half, part)
+        ctx[head, at_half, :, at] = z_rows(head, zl)[...]
 
     rows = 2 * TOK
 
@@ -567,9 +563,9 @@
             pltpu.VMEM((2, SEQ, 128), BF16),
             pltpu.VMEM((4 * TOK, SEQ), F32),
             pltpu.VMEM((4 * TOK, SEQ), F32),
-            pltpu.VMEM((2, 4, 4 * TOK, 128), BF16),
-            pltpu.VMEM((2, 4, 4 * TOK, 128), BF16),
-            pltpu.VMEM((2, 4, TOK, 384), BF16),
+            pltpu.VMEM((2, 4, HEAD_DIM, 640), BF16),
+            pltpu.VMEM((2, 384, 640), BF16),
+            pltpu.VMEM((2, 640, 384), BF16),
             pltpu.VMEM((2, 2, TOK, 768), BF16),
             pltpu.VMEM((2 * TOK, D), F32),
             pltpu.VMEM((2 * TOK, D), BF16),

time: 117 us -> 115 us (0.983)
  Pallas kernels: 115 us -> 113 us
    pallas_call x1, Pallas kernels: 115 us -> 113 us  [layer(): pl.pallas_call(kernel, out_shape=jax.ShapeDtypeStruct((2, TOK, D), BF16),...]
where the time goes in v5:
time: 115 us
  Pallas kernels  113 us (98%)
  local copies, waits for them, and re-layouts  2.03 us (2%)
    pallas_call x1, Pallas kernels, layer(): pl.pallas_call(kernel, out_shape=jax.ShapeDtypeStruct((2, TOK, D), BF16),...  113 us

profile of v5, /device:TPU:1, one launch (start us, length us, event | category | flops | bytes accessed | tf_op | source)
XLA Modules:
  0.0 114.8 jit_solution(5207337835668002152)
XLA Ops:
  0.0 112.7 %shard_map.127 = bf16[2,144,1280]{2,1,0:T(8,128)(2,1)} custom-call(bf16[2,144,1280]{2,1,0:T(8,128)(2,1)} %x_in.1, f32[1280]{0:T(1024)} %pre_gain_in.1, f32[1280]{0:T(1024)} %pre_shift_in.1, f32[3840]{0:T(1024)} %qkv_bias_in.1, f32[1280]{0:T(1024)} %out_bias_in.1, f32[1280]{0:T(1024)} %mlp_gain_in.1, f32[1280]{0:T(1024)} %mlp_shift_in.1, f32[2560]{0:T(1024)} %up_bias_in.1, ...), custom_call_target="tpu_custom_call" | custom-call | tf_op jit(solution)/shard_map/pallas_call | solution.py:544
  112.7 2.0 %copy.15 = bf16[2,144,1280]{2,1,0:T(8,128)(2,1)} copy(bf16[2,144,1280]{2,1,0:T(8,128)(2,1)} %shard_map.127) | data formatting | bytes 1474560
